TPU v7x, 64 devices: a 2x2x8 block of a 4x4x8 slice. The times are simulated.
64 devices in a mesh: dp: 4 (over x, y), sp: 16 (over z, core).
Axes of the slice: x: 2, y: 2, z: 8, core: 2. Of those that a mesh axis runs over, the one named last changes fastest.
The devices are a block of a 4x4x8 slice.
Arguments:
- tok_in: bfloat16 [8192, 5120], P(('dp', 'sp')), parts along dimension 0
- tok_pos: int32 [8192], P(('dp', 'sp')), parts along dimension 0
- w_dq: bfloat16 [5120, 1536], replicated
- g_q: float32 [1536], replicated
- w_uq: bfloat16 [1536, 128, 192], replicated
- w_dkv: bfloat16 [5120, 576], replicated
- g_kv: float32 [512], replicated
- w_uk: bfloat16 [512, 128, 128], replicated
- w_uv: bfloat16 [512, 128, 128], replicated
- w_o: bfloat16 [128, 128, 5120], replicated
Outputs:
- output 1: bfloat16 [8192, 5120], P(('dp', 'sp')), parts along dimension 0
- output 2: bfloat16 [8192, 512], P(('dp', 'sp')), parts along dimension 0
- output 3: bfloat16 [8192, 64], P(('dp', 'sp')), parts along dimension 0
There are 4 independent parts. A program takes and returns all parts, laid end to end along the dimension named above; an argument that names none is the same for every part.
All inputs are finite; a program needn't handle non-finite values.
Results may differ from a plain program's by a relative error of at most 0.0063.
Values are sent between devices in bfloat16 or wider.
A program may use at most 768 MiB of HBM per device.

v0:
```python
import math
import jax
import jax.numpy as jnp
from jax import lax
from jax.sharding import PartitionSpec as P

ROPE_THETA = 10000.0
YARN_FACTOR = 40.0
ORIG_CTX = 4096.0
BETA_FAST = 32.0
BETA_SLOW = 1.0
NORM_EPS = 1e-6


def rope_freqs(rot_dim):
    half_dim = rot_dim // 2
    log_base = 2.0 * math.log(ROPE_THETA)
    low_idx = max(math.floor(rot_dim * math.log(ORIG_CTX / (BETA_FAST * 2.0 * math.pi)) / log_base), 0)
    high_idx = min(math.ceil(rot_dim * math.log(ORIG_CTX / (BETA_SLOW * 2.0 * math.pi)) / log_base), half_dim - 1)
    spread = max(high_idx - low_idx, 0.001)
    freq_list = []
    for freq_idx in range(half_dim):
        base_freq = ROPE_THETA ** (-2.0 * freq_idx / rot_dim)
        ramp_val = min(max((freq_idx - low_idx) / spread, 0.0), 1.0)
        freq_list.append(base_freq / YARN_FACTOR * ramp_val + base_freq * (1.0 - ramp_val))
    return jnp.asarray(freq_list, dtype=jnp.float32)


def rotate_half(act_in, cos_t, sin_t):
    half_dim = act_in.shape[-1] // 2
    first = act_in[..., :half_dim]
    second = act_in[..., half_dim:]
    return jnp.concatenate([first * cos_t - second * sin_t, second * cos_t + first * sin_t], axis=-1)


def rms_norm(act_in, gain):
    mean_sq = jnp.mean(act_in * act_in, axis=-1, keepdims=True)
    return act_in * lax.rsqrt(mean_sq + NORM_EPS) * gain


def solution(mesh):
    groups = mesh.shape['sp']
    tok_spec = P(('dp', 'sp'))
    rows_spec = P(('dp', 'sp'), None)
    replicated = P()

    def local_step(tok_in, tok_pos, w_dq, g_q, w_uq, w_dkv, g_kv, w_uk, w_uv, w_o):
        rows = tok_in.shape[0]
        num_heads = w_uq.shape[1]
        qk_dim = w_uq.shape[2]
        kv_rank = g_kv.shape[0]
        rot_dim = w_dkv.shape[1] - kv_rank
        nope_dim = qk_dim - rot_dim
        v_dim = w_uv.shape[2]
        seq_len = rows * groups
        attn_scale = (0.1 * math.log(YARN_FACTOR) + 1.0) ** 2 / math.sqrt(qk_dim)
        angles = tok_pos.astype(jnp.float32)[:, None] * rope_freqs(rot_dim)[None, :]
        cos_t = jnp.cos(angles)
        sin_t = jnp.sin(angles)
        q_lat = rms_norm(jnp.dot(tok_in, w_dq, preferred_element_type=jnp.float32), g_q).astype(jnp.bfloat16)
        q_full = jnp.einsum('tc,che->the', q_lat, w_uq, preferred_element_type=jnp.float32)
        q_all = jnp.concatenate([q_full[:, :, :nope_dim], rotate_half(q_full[:, :, nope_dim:], cos_t[:, None, :], sin_t[:, None, :])], axis=-1).astype(jnp.bfloat16)
        kv_lat = jnp.dot(tok_in, w_dkv, preferred_element_type=jnp.float32)
        cache_kv = rms_norm(kv_lat[:, :kv_rank], g_kv).astype(jnp.bfloat16)
        cache_pe = rotate_half(kv_lat[:, kv_rank:], cos_t, sin_t).astype(jnp.bfloat16)
        k_nope = jnp.einsum('tc,chn->thn', cache_kv, w_uk, preferred_element_type=jnp.float32).astype(jnp.bfloat16)
        values = jnp.einsum('tc,chv->thv', cache_kv, w_uv, preferred_element_type=jnp.float32).astype(jnp.bfloat16)
        k_all = jnp.concatenate([k_nope, jnp.broadcast_to(cache_pe[:, None, :], (rows, num_heads, rot_dim))], axis=-1)
        q_heads = lax.all_to_all(q_all, 'sp', 1, 0, tiled=True)
        k_heads = lax.all_to_all(k_all, 'sp', 1, 0, tiled=True)
        v_heads = lax.all_to_all(values, 'sp', 1, 0, tiled=True)
        key_idx = jnp.arange(seq_len)

        def block_attention(blk_idx):
            start = blk_idx * rows
            q_blk = lax.dynamic_slice_in_dim(q_heads, start, rows, axis=0)
            logits = jnp.einsum('qhe,khe->hqk', q_blk, k_heads, preferred_element_type=jnp.float32) * attn_scale
            row_idx = start + jnp.arange(rows)
            logits = jnp.where(key_idx[None, None, :] <= row_idx[None, :, None], logits, -jnp.inf)
            attn_prob = jax.nn.softmax(logits, axis=-1).astype(jnp.bfloat16)
            return jnp.einsum('hqk,khv->qhv', attn_prob, v_heads, preferred_element_type=jnp.float32).astype(jnp.bfloat16)

        o_heads = lax.map(block_attention, jnp.arange(groups)).reshape(seq_len, num_heads // groups, v_dim)
        o_local = lax.all_to_all(o_heads, 'sp', 0, 1, tiled=True)
        attn_out = jnp.einsum('thv,hvd->td', o_local, w_o, preferred_element_type=jnp.float32).astype(jnp.bfloat16)
        return attn_out, cache_kv, cache_pe

    return jax.shard_map(local_step, mesh=mesh, in_specs=(rows_spec, tok_spec, replicated, replicated, replicated, replicated, replicated, replicated, replicated, replicated), out_specs=(rows_spec, rows_spec, rows_spec), check_vma=False)
```

profile of v0, /device:TPU:215, one launch (start us, length us, event | category | flops | bytes accessed | tf_op | source)
XLA Modules:
  0.0 889.8 jit_solution(1933614699927694665)
XLA Ops:
  2.0 4.4 fusion.29
  6.6 18.4 %fusion.20 = bf16[128,128,128]{2,0,1:T(8,128)(2,1)} fusion(bf16[512,128,128]{2,1,0:T(8,128)(2,1)} %param.21, bf16[128,512]{0,1:T(8,128)(2,1)S(1)} %multiply_convert_fusion.1), kind=kOutput, calls=%fused_computation.31 | convolution fusion | flops 2149580800 | bytes 21102592 | tf_op jit(solution)/shard_map/tc,chv->thv/dot_general | solution.py:67
  25.0 6.3 all-to-all-start.2
  31.3 7.8 multiply_reduce_fusion
  39.1 74.7 %fusion.15 = f32[128,128,192]{1,0,2:T(8,128)} fusion(bf16[1536,128,192]{1,2,0:T(8,128)(2,1)} %param.17, f32[128,1536]{1,0:T(8,128)S(1)} %get-tuple-element.88, f32[1536]{0:T(1024)S(1)} %copy-done.6, f32[128]{0:T(128)S(1)} %add_rsqrt_fusion.1), kind=kOutput, calls=%fused_computation.20 | convolution fusion | flops 9664266240 | bytes 88873472 | tf_op jit(solution)/shard_map/tc,che->the/dot_general | solution.py:61
  113.7 4.4 slice.48
  121.9 17.4 %pad_maximum_fusion = bf16[128,128,192]{1,0,2:T(8,128)(2,1)} fusion(bf16[128,128,32]{1,0,2:T(8,128)(2,1)S(1)} %get-tuple-element.82, bf16[128,128,32]{1,0,2:T(8,128)(2,1)S(1)} %get-tuple-element.81, bf16[128,128,128]{1,0,2:T(8,128)(2,1)S(1)} %slice.48), kind=kLoop, calls=%fused_computation.27 | loop fusion | flops 6291456 | bytes 12582912 | tf_op jit(solution)/shard_map/concatenate | solution.py:62
  139.3 9.0 %copy.47 = bf16[128,128,192]{0,2,1:T(8,128)(2,1)} copy(bf16[128,128,192]{1,0,2:T(8,128)(2,1)} %pad_maximum_fusion) | data formatting | bytes 12582912 | tf_op jit(solution)/shard_map/concatenate | solution.py:62
  148.3 7.2 all-to-all-start
  155.5 24.4 %copy.50 = bf16[512,128,128]{0,2,1:T(8,128)(2,1)} copy(bf16[512,128,128]{2,1,0:T(8,128)(2,1)} %param.20) | data formatting | bytes 33554432 | tf_op args[7]
  179.9 8.1 fusion.30
  193.3 101.9 %all-to-all-done = bf16[128,128,192]{0,2,1:T(8,128)(2,1)} async-done(((bf16[128,128,192]{0,2,1:T(8,128)(2,1)}), bf16[128,128,192]{0,2,1:T(8,128)(2,1)}, u32[]{:S(2)}, u32[]{:S(2)}) %all-to-all-start) | async-done | bytes 6291488 | tf_op jit(solution)/shard_map/all_to_all | solution.py:69
  295.3 10.4 %all-to-all-start.1 = ((bf16[128,128,192]{0,2,1:T(8,128)(2,1)}), bf16[128,128,192]{0,2,1:T(8,128)(2,1)}, u32[]{:S(2)}, u32[]{:S(2)}) async-start(bf16[128,128,192]{0,2,1:T(8,128)(2,1)} %pad_maximum_fusion.1), calls=%async_computation.1 | async-start | bytes 12582912 | tf_op jit(solution)/shard_map/all_to_all | solution.py:70
  305.6 4.7 copy.54
  310.3 7.2 copy.75
  317.6 127.8 %all-to-all-done.1 = bf16[128,128,192]{0,2,1:T(8,128)(2,1)} async-done(((bf16[128,128,192]{0,2,1:T(8,128)(2,1)}), bf16[128,128,192]{0,2,1:T(8,128)(2,1)}, u32[]{:S(2)}, u32[]{:S(2)}) %all-to-all-start.1) | async-done | bytes 6291488 | tf_op jit(solution)/shard_map/all_to_all | solution.py:70
  445.4 7.1 copy.74
  452.5 273.3 %while.11 = (s32[]{:T(128)}, bf16[16,128,8,128]{3,2,1,0:T(8,128)(2,1)}, s32[16]{0:T(128)S(1)}, bf16[2048,8,192]{0,2,1:T(8,128)(2,1)}, bf16[2048,8,192]{0,2,1:T(8...) while((s32[]{:T(128)}, ...), condition=%wide.region_5.6_spmd.clone, body=%wide.region_2.5_spmd.clone.sunk | while | flops 1359349888 | bytes 62531264 | solution.py:83
  453.8 4.2 fusion.50
  458.3 5.7 fusion.51
  463.9 4.8 fusion.52
  470.9 4.2 fusion.50
  475.3 5.7 fusion.51
  481.0 4.8 fusion.52
  487.9 4.2 fusion.50
  492.4 5.7 fusion.51
  498.1 4.8 fusion.52
  505.0 4.2 fusion.50
  509.5 5.7 fusion.51
  515.2 4.8 fusion.52
  526.6 5.7 fusion.51
  532.2 4.8 fusion.52
  539.1 4.2 fusion.50
  543.6 5.7 fusion.51
  549.3 4.8 fusion.52
  556.2 4.2 fusion.50
  560.7 5.7 fusion.51
  566.4 4.8 fusion.52
  573.3 4.2 fusion.50
  577.8 5.7 fusion.51
  583.5 4.8 fusion.52
  590.4 4.2 fusion.50
  594.9 5.7 fusion.51
  600.5 4.8 fusion.52
  611.9 5.7 fusion.51
  617.6 4.8 fusion.52
  624.5 4.2 fusion.50
  629.0 5.7 fusion.51
  634.7 4.8 fusion.52
  641.6 4.2 fusion.50
  646.1 5.7 fusion.51
  651.8 4.8 fusion.52
  663.2 5.7 fusion.51
  668.8 4.8 fusion.52
  680.3 5.7 fusion.51
  685.9 4.8 fusion.52
  697.4 5.7 fusion.51
  703.0 4.8 fusion.52
  714.4 5.7 fusion.51
  720.1 4.8 fusion.52
  725.8 10.4 %all-to-all-start.3 = ((bf16[2048,8,128]{2,1,0:T(8,128)(2,1)}), bf16[2048,8,128]{2,1,0:T(8,128)(2,1)}, u32[]{:S(2)}, u32[]{:S(2)}) async-start(bf16[2048,8,128]{2,1,0:T(8,128)(2,1)} %bitcast.11), calls=%async_computation.3 | async-start | bytes 8388608 | tf_op jit(solution)/shard_map/all_to_all | solution.py:84
  736.9 91.9 %all-to-all-done.3 = bf16[2048,8,128]{2,1,0:T(8,128)(2,1)} async-done(((bf16[2048,8,128]{2,1,0:T(8,128)(2,1)}), bf16[2048,8,128]{2,1,0:T(8,128)(2,1)}, u32[]{:S(2)}, u32[]{:S(2)}) %all-to-all-start.3) | async-done | bytes 4194336 | tf_op jit(solution)/shard_map/all_to_all | solution.py:84
  828.8 5.4 copy.56
  834.2 55.4 %fusion.19 = bf16[128,5120]{1,0:T(8,128)(2,1)} fusion(bf16[128,128,128]{2,0,1:T(8,128)(2,1)} %bitcast.61, bf16[128,128,5120]{2,1,0:T(8,128)(2,1)} %param.22), kind=kOutput, calls=%fused_computation.30 | convolution fusion | flops 21475491840 | bytes 173277184 | tf_op jit(solution)/shard_map/thv,hvd->td/dot_general | solution.py:85
  (131 shorter events, 63.8 us)
Async XLA Ops:
  0.6 1.3 copy-start
  0.6 5.8 copy-start.4
  25.0 6.3 copy-start.7
  25.0 123.3 %all-to-all-start.2 = ((bf16[128,128,128]{2,0,1:T(8,128)(2,1)}), bf16[128,128,128]{2,0,1:T(8,128)(2,1)}, u32[]{:S(2)}, u32[]{:S(2)}) async-start(bf16[128,128,128]{2,0,1:T(8,128)(2,1)} %fusion.20), calls=%async_computation.2 | async-start | bytes 8388608 | tf_op jit(solution)/shard_map/all_to_all | solution.py:71
  31.3 7.8 copy-start.6
  113.7 4.4 copy-start.5
  148.3 147.0 %all-to-all-start = ((bf16[128,128,192]{0,2,1:T(8,128)(2,1)}), bf16[128,128,192]{0,2,1:T(8,128)(2,1)}, u32[]{:S(2)}, u32[]{:S(2)}) async-start(bf16[128,128,192]{0,2,1:T(8,128)(2,1)} %copy.47), calls=%async_computation | async-start | bytes 12582912 | tf_op jit(solution)/shard_map/all_to_all | solution.py:69
  189.0 0.6 copy-start.3
  295.3 150.1 %all-to-all-start.1 = ((bf16[128,128,192]{0,2,1:T(8,128)(2,1)}), bf16[128,128,192]{0,2,1:T(8,128)(2,1)}, u32[]{:S(2)}, u32[]{:S(2)}) async-start(bf16[128,128,192]{0,2,1:T(8,128)(2,1)} %pad_maximum_fusion.1), calls=%async_computation.1 | async-start | bytes 12582912 | tf_op jit(solution)/shard_map/all_to_all | solution.py:70
  458.2 5.7 copy-start.2
  475.3 5.7 copy-start.2
  492.4 5.7 copy-start.2
  509.5 5.7 copy-start.2
  526.6 5.7 copy-start.2
  543.6 5.7 copy-start.2
  560.7 5.7 copy-start.2
  577.8 5.7 copy-start.2
  594.8 5.7 copy-start.2
  611.9 5.7 copy-start.2
  629.0 5.7 copy-start.2
  646.1 5.7 copy-start.2
  663.2 5.7 copy-start.2
  680.2 5.7 copy-start.2
  697.3 5.7 copy-start.2
  714.4 5.7 copy-start.2
  725.8 103.0 %all-to-all-start.3 = ((bf16[2048,8,128]{2,1,0:T(8,128)(2,1)}), bf16[2048,8,128]{2,1,0:T(8,128)(2,1)}, u32[]{:S(2)}, u32[]{:S(2)}) async-start(bf16[2048,8,128]{2,1,0:T(8,128)(2,1)} %bitcast.11), calls=%async_computation.3 | async-start | bytes 8388608 | tf_op jit(solution)/shard_map/all_to_all | solution.py:84
  834.2 55.4 %copy-start.1 = (bf16[128,5120]{1,0:T(8,128)(2,1)S(1)}, bf16[128,5120]{1,0:T(8,128)(2,1)}, u32[]{:S(2)}) copy-start(bf16[128,5120]{1,0:T(8,128)(2,1)} %param.13) | copy-start | bytes 3932164
where the time goes:
time: 899 us; the launch traced here: 890 us
  waiting for transfers between devices  322 us (36%)
  matrix products  313 us (35%)
  other arithmetic  120 us (13%)
  local copies, waits for them, and re-layouts  88.9 us (10%)
  starting transfers between devices  34.3 us (4%)
  loops' own time  11.1 us (1%)
    all_to_all x1, waiting for transfers between devices, local_step(): k_heads = lax.all_to_all(k_all, 'sp', 1, 0, tiled=True)  128 us
    all_to_all x1, waiting for transfers between devices, local_step(): q_heads = lax.all_to_all(q_all, 'sp', 1, 0, tiled=True)  102 us
    all_to_all x1, waiting for transfers between devices, local_step(): o_local = lax.all_to_all(o_heads, 'sp', 0, 1, tiled=True)  91.9 us
    sub x16, other arithmetic, block_attention(): attn_prob = jax.nn.softmax(logits, axis=-1).astype(jnp.bfloat16)  90.8 us
    dot_general x16, matrix products, block_attention(): jnp.einsum('hqk,khv->qhv', attn_prob, v_heads, preferred_element_type=jnp...  76.4 us
    dot_general x1, matrix products, local_step(): jnp.einsum('tc,che->the', q_lat, w_uq, preferred_element_type=jnp.float32)  74.7 us
    dot_general x16, matrix products, block_attention(): jnp.einsum('qhe,khe->hqk', q_blk, k_heads, preferred_element_type=jnp.flo...  67.9 us
    dot_general x1, matrix products, local_step(): jnp.einsum('thv,hvd->td', o_local, w_o, preferred_element_type=jnp.float32)  55.4 us
  transfers between devices with their start and end apart: 4, of which 3 were waited for; matrix products, arithmetic and copies ran while one was open for 19% of the time, Pallas kernels for 0%

commit v1 on v0

v1 whole, which is shorter than its diff:
```python
import functools
import math

import jax
import jax.numpy as jnp
from jax import lax
from jax.experimental import pallas as pl
from jax.experimental.pallas import tpu as pltpu
from jax.sharding import PartitionSpec as P

ROPE_THETA = 10000.0
YARN_FACTOR = 40.0
ORIG_CTX = 4096.0
BETA_FAST = 32.0
BETA_SLOW = 1.0
NORM_EPS = 1e-6

MESH = pl.DeviceIdType.MESH
F32 = jnp.float32
BF16 = jnp.bfloat16


def rope_freqs(rot_dim):
    half_dim = rot_dim // 2
    log_base = 2.0 * math.log(ROPE_THETA)
    low_idx = max(math.floor(rot_dim * math.log(ORIG_CTX / (BETA_FAST * 2.0 * math.pi)) / log_base), 0)
    high_idx = min(math.ceil(rot_dim * math.log(ORIG_CTX / (BETA_SLOW * 2.0 * math.pi)) / log_base), half_dim - 1)
    spread = max(high_idx - low_idx, 0.001)
    freq_list = []
    for freq_idx in range(half_dim):
        base_freq = ROPE_THETA ** (-2.0 * freq_idx / rot_dim)
        ramp_val = min(max((freq_idx - low_idx) / spread, 0.0), 1.0)
        freq_list.append(base_freq / YARN_FACTOR * ramp_val + base_freq * (1.0 - ramp_val))
    return jnp.asarray(freq_list, dtype=jnp.float32)


def rotate_half(act_in, cos_t, sin_t):
    half_dim = act_in.shape[-1] // 2
    first = act_in[..., :half_dim]
    second = act_in[..., half_dim:]
    return jnp.concatenate([first * cos_t - second * sin_t, second * cos_t + first * sin_t], axis=-1)


def rms_norm(act_in, gain):
    mean_sq = jnp.mean(act_in * act_in, axis=-1, keepdims=True)
    return act_in * lax.rsqrt(mean_sq + NORM_EPS) * gain


def dot(a, b):
    return jnp.dot(a, b, preferred_element_type=F32)


def mla_kernel(cfg, cblk, cqT, trig, wq, wk, wv, wo, out,
               c_all, cq_all, trig_all, cT, kcat, vT, q_scr, o_all, acc_o, acc, stage, fin,
               wq_buf, wk_buf, wv_buf, wo_buf,
               sendR, recvR, sendL, recvL, sendD, recvD, sendX, recvX, send_o, recv_o, send_f, recv_f,
               wq_sem, wk_sem, wv_sem, wo_sem):
    Z, T, C, NOPE, ROPE, V, H = cfg["Z"], cfg["T"], cfg["C"], cfg["NOPE"], cfg["ROPE"], cfg["V"], cfg["H"]
    CH, HB, D, scale2 = cfg["CH"], cfg["HB"], cfg["D"], cfg["scale2"]
    NQB, NOB = wq_buf.shape[0], wo_buf.shape[0]
    HC = H // 2
    NU = HC // 2
    DC = D // 2
    W = 2 * T
    QK = NOPE + ROPE
    half = ROPE // 2
    NR, NL = Z // 2, (Z - 1) // 2

    idx = lax.axis_index("sp")
    z, core = idx // 2, lax.rem(idx, 2)
    right = lax.rem(z + 1, Z) * 2 + core
    left = lax.rem(z + Z - 1, Z) * 2 + core
    other = z * 2 + (1 - core)

    def rows_of(chip_off):
        blk = lax.rem(z + chip_off + 2 * Z, Z) * 2 + core
        return pl.ds(pl.multiple_of(blk * T, T), T)

    barrier = pltpu.get_barrier_semaphore()
    for dev in (left, right, other):
        pl.semaphore_signal(barrier, inc=1, device_id={"sp": dev}, device_id_type=MESH)
    pl.semaphore_wait(barrier, 3)

    def remote(src, dst, ssem, rsem, dev):
        return pltpu.make_async_remote_copy(src_ref=src, dst_ref=dst, send_sem=ssem, recv_sem=rsem,
                                            device_id={"sp": dev}, device_id_type=MESH)

    own = rows_of(0)

    def right_copy(s):
        rows = rows_of(-s)
        return remote(cblk if s == 0 else c_all.at[rows], c_all.at[rows], sendR.at[s], recvR.at[s], right)

    def left_copy(s):
        rows = rows_of(s)
        return remote(cblk if s == 0 else c_all.at[rows], c_all.at[rows], sendL.at[s], recvL.at[s], left)

    def pair_copy(s):
        if s == 0:
            rows, src = own, cblk
        else:
            rows = rows_of(-s) if s <= NR else rows_of(s - NR)
            src = c_all.at[rows]
        return remote(src, c_all.at[rows], sendD.at[s], recvD.at[s], other)

    cq_copy = remote(cqT, cq_all.at[core], sendX.at[0], recvX.at[0], other)
    trig_copy = remote(trig, trig_all.at[core], sendX.at[1], recvX.at[1], other)
    cq_copy.start()
    trig_copy.start()
    right_copy(0).start()
    left_copy(0).start()
    pair_copy(0).start()

    def wq_copy(u):
        h0 = core * HC + 2 * u
        return pltpu.make_async_copy(wq.at[pl.ds(h0, 2)], wq_buf.at[lax.rem(u, NQB)], wq_sem.at[lax.rem(u, NQB)])

    def wkv_copies(u):
        h0 = core * HC + 2 * u
        p = lax.rem(u, 2)
        return (pltpu.make_async_copy(wk.at[pl.ds(h0, 2)], wk_buf.at[p], wk_sem.at[p]),
                pltpu.make_async_copy(wv.at[pl.ds(h0, 2)], wv_buf.at[p], wv_sem.at[p]))

    def wo_copy(i):
        hb = lax.rem(core * (HC // HB) + i, H // HB)
        src = wo.at[pl.ds(pl.multiple_of(hb * HB * V, HB * V), HB * V), pl.ds(pl.multiple_of(core * DC, DC), DC)]
        return pltpu.make_async_copy(src, wo_buf.at[lax.rem(i, NOB)], wo_sem.at[lax.rem(i, NOB)])

    for u in range(min(NQB, NU)):
        wq_copy(u).start()

    c_all[own, :] = cblk[...]
    cq_all[core] = cqT[...]
    trig_all[core] = trig[...]
    cq_copy.wait_recv()
    trig_copy.wait_recv()

    cosT = jnp.concatenate([trig_all[0, :half], trig_all[1, :half]], axis=1)
    sinT = jnp.concatenate([trig_all[0, half:], trig_all[1, half:]], axis=1)

    def q_unit(u, carry):
        slot = lax.rem(u, NQB)
        wq_copy(u).wait()
        w2 = wq_buf[slot].reshape(2 * QK, wq_buf.shape[3])
        cqs = jnp.concatenate([cq_all[0], cq_all[1]], axis=1)
        q = dot(w2, cqs)
        for h in range(2):
            b = h * QK
            z1, z2 = q[b + NOPE:b + NOPE + half], q[b + NOPE + half:b + QK]
            q_scr[u, h, :NOPE] = q[b:b + NOPE].astype(BF16)
            q_scr[u, h, NOPE:NOPE + half] = (z1 * cosT - z2 * sinT).astype(BF16)
            q_scr[u, h, NOPE + half:QK] = (z2 * cosT + z1 * sinT).astype(BF16)
            q_scr[u, h, QK:] = jnp.zeros((q_scr.shape[2] - QK, W), BF16)

        @pl.when(u + NQB < NU)
        def _():
            wq_copy(u + NQB).start()
        return carry

    cuts = [NU * s // NR for s in range(NR + 1)]
    for s in range(NR):
        lax.fori_loop(cuts[s], cuts[s + 1], q_unit, 0)
        right_copy(s).wait_recv()
        if s + 1 < NR:
            right_copy(s + 1).start()
        pair_copy(s + 1).start()
        if s < NL:
            left_copy(s).wait_recv()
            if s + 1 < NL:
                left_copy(s + 1).start()
            pair_copy(1 + NR + s).start()

    for c in wkv_copies(0) + wkv_copies(1):
        c.start()
    for i in range(NOB):
        wo_copy(i).start()
    for s in range(1 + NR + NL):
        pair_copy(s).wait_recv()

    nch = (W * z) // CH + 1

    def transpose_chunk(j, carry):
        cT[j] = c_all[pl.ds(pl.multiple_of(j * CH, CH), CH), :C].T
        return carry

    lax.fori_loop(0, nch, transpose_chunk, 0)

    def make_kv(u, j, slot):
        p = lax.rem(u, 2)
        cc = c_all[pl.ds(pl.multiple_of(j * CH, CH), CH), :C]
        pe = c_all[pl.ds(pl.multiple_of(j * CH, CH), CH), C:]
        k2 = dot(cc, jnp.concatenate([wk_buf[p, 0], wk_buf[p, 1]], axis=1)).astype(BF16)
        for h in range(2):
            kcat[slot, h, :, :NOPE] = k2[:, h * NOPE:(h + 1) * NOPE]
            kcat[slot, h, :, NOPE:] = pe
        vT[slot] = dot(wv_buf[p].reshape(2 * V, C), cT[j]).astype(BF16)

    def body(u, j, t, un, jn, ml, masked):
        slot, nslot = lax.rem(t, 2), lax.rem(t + 1, 2)
        s = [dot(kcat[slot, h], q_scr[u, h]) for h in range(2)]
        make_kv(un, jn, nslot)
        out = []
        for h in range(2):
            m, l = ml[h]
            sh = s[h]
            if masked:
                kk = lax.broadcasted_iota(jnp.int32, (CH, W), 0)
                qq = lax.broadcasted_iota(jnp.int32, (CH, W), 1)
                sh = jnp.where(kk - qq <= W * z - CH * j, sh, -jnp.inf)
            mn = jnp.maximum(m, jnp.max(sh, axis=0, keepdims=True))
            alpha = jnp.exp2((m - mn) * scale2)
            p = jnp.exp2((sh - mn) * scale2)
            ln = l * alpha + jnp.sum(p, axis=0, keepdims=True)
            acc_o[h] = acc_o[h] * alpha + dot(vT[slot, h * V:(h + 1) * V], p.astype(BF16))
            out.append((mn, ln))
        return tuple(out)

    def o_copy(u):
        unit = core * NU + u
        return remote(o_all.at[unit], o_all.at[unit], send_o.at[u], recv_o.at[u], other)

    for c in wkv_copies(0):
        c.wait()
    make_kv(0, 0, 0)

    def attn_unit(u, carry):
        t0 = u * nch
        acc_o[...] = jnp.zeros(acc_o.shape, F32)
        init = tuple((jnp.full((1, W), -1e30, F32), jnp.zeros((1, W), F32)) for _ in range(2))
        ml = lax.fori_loop(0, nch - 1, lambda j, ml: body(u, j, t0 + j, u, j + 1, ml, False), init)

        @pl.when(u + 1 < NU)
        def _():
            for c in wkv_copies(u + 1):
                c.wait()

        @pl.when(u + 2 < NU)
        def _():
            for c in wkv_copies(u + 2):
                c.start()

        @pl.when(u > 0)
        def _():
            o_copy(u - 1).start()

        ml = body(u, nch - 1, t0 + nch - 1, lax.rem(u + 1, NU), 0, ml, True)
        for h in range(2):
            o_all[core * NU + u, :, h * V:(h + 1) * V] = (acc_o[h] * (1.0 / ml[h][1])).T.astype(BF16)
        return carry

    lax.fori_loop(0, NU, attn_unit, 0)

    NB = H // HB
    CT = DC // 5 if DC % 640 == 0 else DC

    def out_block(i, first):
        hb = lax.rem(core * (HC // HB) + i, NB)
        slot = lax.rem(i, NOB)
        wo_copy(i).wait()
        ob = jnp.concatenate([o_all[hb * (HB // 2) + g] for g in range(HB // 2)], axis=1)
        for r in range(DC // CT):
            cs = slice(r * CT, (r + 1) * CT)
            d = dot(ob, wo_buf[slot, :, cs])
            if first:
                acc[:, cs] = d
            else:
                acc[:, cs] = acc[:, cs] + d

        @pl.when(i + NOB < NB)
        def _():
            wo_copy(i + NOB).start()

    out_block(0, True)
    o_copy(NU - 1).start()

    def own_block(i, carry):
        out_block(i, False)
        return carry

    def far_block(i, carry):
        for g in range(HB // 2):
            o_copy((i - NB // 2) * (HB // 2) + g).wait_recv()
        out_block(i, False)
        return carry

    lax.fori_loop(1, NB // 2, own_block, 0)
    lax.fori_loop(NB // 2, NB, far_block, 0)

    stage[...] = acc[pl.ds(pl.multiple_of((1 - core) * T, T), T), :].astype(BF16)
    final = remote(stage, fin, send_f, recv_f, other)
    final.start()
    out[:, pl.ds(pl.multiple_of(core * DC, DC), DC)] = acc[pl.ds(pl.multiple_of(core * T, T), T), :].astype(BF16)
    final.wait_recv()
    out[:, pl.ds(pl.multiple_of((1 - core) * DC, DC), DC)] = fin[...]

    for s in range(NR):
        right_copy(s).wait_send()
    for s in range(NL):
        left_copy(s).wait_send()
    for s in range(1 + NR + NL):
        pair_copy(s).wait_send()
    cq_copy.wait_send()
    trig_copy.wait_send()

    def drain(u, carry):
        o_copy(u).wait_send()
        return carry

    lax.fori_loop(0, NU, drain, 0)
    final.wait_send()


def solution(mesh):
    groups = mesh.shape["sp"]
    tok_spec = P(("dp", "sp"))
    rows_spec = P(("dp", "sp"), None)
    rep = P()

    def local_step(tok_in, tok_pos, w_dq, g_q, w_uq, w_dkv, g_kv, w_uk, w_uv, w_o):
        T, D = tok_in.shape
        CQ, H, QK = w_uq.shape
        C = g_kv.shape[0]
        ROPE = w_dkv.shape[1] - C
        NOPE = QK - ROPE
        V = w_uv.shape[2]
        Z = groups // 2
        seq = T * groups
        W = 2 * T
        CH = 2 * W
        HB = min(8, H // 2)
        NU = H // 4
        NCH = seq // CH
        KD = 2 * NOPE
        attn_scale = (0.1 * math.log(YARN_FACTOR) + 1.0) ** 2 / math.sqrt(QK)

        angles = tok_pos.astype(F32)[:, None] * rope_freqs(ROPE)[None, :]
        cos_t = jnp.cos(angles)
        sin_t = jnp.sin(angles)
        q_lat = rms_norm(jnp.dot(tok_in, w_dq, preferred_element_type=F32), g_q).astype(BF16)
        kv_lat = jnp.dot(tok_in, w_dkv, preferred_element_type=F32)
        cache_kv = rms_norm(kv_lat[:, :C], g_kv).astype(BF16)
        cache_pe = rotate_half(kv_lat[:, C:], cos_t, sin_t).astype(BF16)

        cblk = jnp.concatenate([cache_kv, cache_pe, jnp.zeros((T, KD - NOPE - ROPE), BF16)], axis=1)
        trig = jnp.concatenate([cos_t.T, sin_t.T], axis=0)
        cfg = dict(Z=Z, T=T, C=C, NOPE=NOPE, ROPE=ROPE, V=V, H=H, CH=CH, HB=HB, D=D, scale2=attn_scale * math.log2(math.e))
        NQB, NOB = 4, min(4, H // HB)
        NR, NL = Z // 2, (Z - 1) // 2
        dma = pltpu.SemaphoreType.DMA
        vm = pl.BlockSpec(memory_space=pltpu.VMEM)
        hbm = pl.BlockSpec(memory_space=pltpu.HBM)
        attn_out = pl.pallas_call(
            functools.partial(mla_kernel, cfg),
            out_shape=jax.ShapeDtypeStruct((T, D), BF16),
            in_specs=[vm, vm, vm, hbm, hbm, hbm, hbm],
            out_specs=vm,
            scratch_shapes=[
                pltpu.VMEM((seq, C + KD - NOPE), BF16),
                pltpu.VMEM((2, CQ, T), BF16),
                pltpu.VMEM((2, ROPE, T), F32),
                pltpu.VMEM((NCH, C, CH), BF16),
                pltpu.VMEM((2, 2, CH, KD), BF16),
                pltpu.VMEM((2, 2 * V, CH), BF16),
                pltpu.VMEM((NU, 2, KD, W), BF16),
                pltpu.VMEM((H // 2, W, 2 * V), BF16),
                pltpu.VMEM((2, V, W), F32),
                pltpu.VMEM((W, D // 2), F32),
                pltpu.VMEM((T, D // 2), BF16),
                pltpu.VMEM((T, D // 2), BF16),
                pltpu.VMEM((NQB, 2, QK, CQ), BF16),
                pltpu.VMEM((2, 2, C, NOPE), BF16),
                pltpu.VMEM((2, 2, V, C), BF16),
                pltpu.VMEM((NOB, HB * V, D // 2), BF16),
                dma((NR,)), dma((NR,)), dma((max(NL, 1),)), dma((max(NL, 1),)), dma((1 + NR + NL,)), dma((1 + NR + NL,)),
                dma((2,)), dma((2,)), dma((NU,)), dma((NU,)), dma, dma,
                dma((NQB,)), dma((2,)), dma((2,)), dma((NOB,)),
            ],
            compiler_params=pltpu.CompilerParams(collective_id=0, has_side_effects=True, vmem_limit_bytes=66_000_000),
            name="mla",
        )(cblk, q_lat.T, trig, jnp.transpose(w_uq, (1, 2, 0)), jnp.transpose(w_uk, (1, 0, 2)),
          jnp.transpose(w_uv, (1, 2, 0)), w_o.reshape(H * V, D))
        return attn_out, cache_kv, cache_pe

    return jax.shard_map(local_step, mesh=mesh, in_specs=(rows_spec, tok_spec) + (rep,) * 8,
                         out_specs=(rows_spec, rows_spec, rows_spec), check_vma=False)
```

time: 899 us -> 343 us (0.38)
  waiting for transfers between devices: 322 us -> 0 us
  matrix products: 313 us -> 13 us
  Pallas kernels: 0 us -> 172 us
  other arithmetic: 120 us -> 4.56 us
  local copies, waits for them, and re-layouts: 88.9 us -> 148 us
  starting transfers between devices: 34.3 us -> 0 us
  loops' own time: 11.1 us -> 0 us
    all_to_all x4 -> x0, waiting for transfers between devices: 322 us -> none  [the longest x1 128 us: local_step(): k_heads = lax.all_to_all(k_all, 'sp', 1, 0, tiled=True)]
    dot_general x37 -> x2, matrix products: 305 us -> 13 us  [the longest x1 7.77 us: local_step(): jnp.dot(tok_in, w_dq, preferred_element_type=F32)]
    pallas_call x0 -> x1, Pallas kernels: none -> 172 us  [local_step(): pl.pallas_call(functools.partial(mla_kernel, cfg), out_shape=jax.ShapeDty...]
    unnamed x16 -> x15, local copies, waits for them, and re-layouts: 27.1 us -> 148 us
    sub x16 -> x0, other arithmetic: 90.8 us -> none  [block_attention(): attn_prob = jax.nn.softmax(logits, axis=-1).astype(jnp.bfloat16)]
    all_to_all x4 -> x0, starting transfers between devices: 34.3 us -> none  [the longest x1 10.4 us: local_step(): k_heads = lax.all_to_all(k_all, 'sp', 1, 0, tiled=True)]
    all_to_all x4 -> x0, local copies, waits for them, and re-layouts: 24.5 us -> none  [the longest x1 7.25 us: local_step(): q_heads = lax.all_to_all(q_all, 'sp', 1, 0, tiled=True)]
    concatenate x2, other arithmetic: 20.6 us -> 1.37 us  [the longest x1 0.76 us: local_step(): jnp.concatenate([cache_kv, cache_pe, jnp.zeros((T, KD - NOPE - ROPE), BF1...]
  transfers between devices with their start and end apart: 4 -> 0, of which waited for: 3 -> 0; matrix products, arithmetic and copies ran while one was open for 19% -> 0% of each run, Pallas kernels for 0% -> 0%
where the time goes in v1:
time: 343 us; the launch traced here: 339 us
  Pallas kernels  172 us (50%)
  local copies, waits for them, and re-layouts  148 us (43%)
  matrix products  13 us (4%)
  other arithmetic  4.56 us (1%)
    pallas_call x1, Pallas kernels, local_step(): pl.pallas_call(functools.partial(mla_kernel, cfg), out_shape=jax.ShapeDty...  172 us
    unnamed x15, local copies, waits for them, and re-layouts  148 us
    dot_general x1, matrix products, local_step(): jnp.dot(tok_in, w_dq, preferred_element_type=F32)  7.77 us

profile of v1, /device:TPU:215, one launch (start us, length us, event | category | flops | bytes accessed | tf_op | source)
XLA Modules:
  0.0 339.1 jit_solution(14874259424521212715)
XLA Ops:
  0.6 0.0 copy-start.4
  0.6 0.0 copy-start
  0.7 0.0 copy-start.3
  0.7 0.8 convert_element_type.15
  1.4 0.1 pad.7.clone
  1.5 0.8 multiply_cosine_fusion.1
  2.3 0.6 pad_maximum_fusion.trig
  2.9 5.2 %fusion.9 = f32[128,576]{1,0:T(8,128)S(1)} fusion(bf16[128,5120]{1,0:T(8,128)(2,1)} %param.11, bf16[5120,576]{0,1:T(8,128)(2,1)} %param.16), kind=kOutput, calls=%fused_computation.23 | convolution fusion | flops 754974720 | bytes 7503872 | tf_op jit(solution)/shard_map/dot_general | solution.py:340
  8.1 0.1 multiply_reduce_fusion.1
  8.3 0.0 copy-done.4
  8.3 0.3 fusion.6
  8.6 0.0 copy-done.3
  8.6 0.1 multiply_convert_fusion.1
  8.7 0.0 copy-start.1
  8.7 0.1 pad_maximum_fusion.1
  8.8 0.7 copy.30
  9.5 0.8 maximum_maximum_fusion.cblk
  10.3 0.0 copy-done
  10.3 0.0 copy-start.2
  10.3 7.8 %multiply_reduce_fusion = (f32[128]{0:T(128)S(1)}, f32[128,1536]{1,0:T(8,128)S(1)}) fusion(bf16[128,5120]{1,0:T(8,128)(2,1)S(1)} %copy-done, bf16[5120,1536]{1,0:T(8,128)(2,1)} %param.13), kind=kOutput, calls=%fused_computation.2 | convolution fusion | flops 2013659008 | bytes 17826304 | tf_op jit(solution)/shard_map/dot_general | solution.py:339
  18.0 0.0 copy-done.1
  18.1 0.3 copy.26
  18.3 0.0 copy-done.2
  18.3 1.0 fusion.cqT
  19.3 16.8 %copy.33 = bf16[512,128,128]{2,0,1:T(8,128)(2,1)} copy(bf16[512,128,128]{2,1,0:T(8,128)(2,1)} %param.18) | data formatting | bytes 33554432 | tf_op args[7]
  36.1 24.7 %copy.29 = bf16[512,128,128]{0,2,1:T(8,128)(2,1)} copy(bf16[512,128,128]{2,1,0:T(8,128)(2,1)} %param.19) | data formatting | bytes 33554432 | tf_op args[8]
  60.8 103.5 %copy.27 = bf16[1536,128,192]{0,2,1:T(8,128)(2,1)} copy(bf16[1536,128,192]{1,2,0:T(8,128)(2,1)} %param.15) | data formatting | bytes 150994944 | tf_op args[4]
  164.3 172.4 %mla.1 = bf16[128,5120]{1,0:T(8,128)(2,1)} custom-call(bf16[128,640]{1,0:T(8,128)(2,1)} %maximum_maximum_fusion.cblk, bf16[1536,128]{1,0:T(8,128)(2,1)} %fusion.cqT, f32[64,128]{1,0:T(8,128)} %pad_maximum_fusion.trig, bf16[128,192,1536]{2,1,0:T(8,128)(2,1)} %bitcast.1.wq, bf16[128,512,128]{2,1,0:T(8,128)(2,1)} %bitcast.12, bf16[128,128,512]{2,1,0:T(8,128)(2,1)} %bitcast.13, ...), custom_call_target="tpu_custom_call" | custom-call | tf_op jit(solution)/shard_map/mla/pallas_call | solution.py:352
  336.7 2.5 copy.35
  (3 shorter events, 0.0 us)
Async XLA Ops:
  0.6 7.6 %copy-start.4 = (f32[32]{0:T(128)S(1)}, f32[32]{0:T(128)}, u32[]{:S(2)}) copy-start(f32[32]{0:T(128)} %constant.14.clone) | copy-start | bytes 388
  0.6 9.6 %copy-start = (bf16[128,5120]{1,0:T(8,128)(2,1)S(1)}, bf16[128,5120]{1,0:T(8,128)(2,1)}, u32[]{:S(2)}) copy-start(bf16[128,5120]{1,0:T(8,128)(2,1)} %param.11) | copy-start | bytes 3932164
  0.7 7.9 %copy-start.3 = (f32[512]{0:T(512)S(1)}, f32[512]{0:T(512)}, u32[]{:S(2)}) copy-start(f32[512]{0:T(512)} %param.17) | copy-start | bytes 6148
  8.7 9.3 %copy-start.1 = (bf16[128,512]{1,0:T(8,128)(2,1)}, bf16[128,512]{1,0:T(8,128)(2,1)S(1)}, u32[]{:S(2)}) copy-start(bf16[128,512]{1,0:T(8,128)(2,1)S(1)} %multiply_convert_fusion.1) | copy-start | bytes 393220
  10.3 8.1 %copy-start.2 = (f32[1536]{0:T(1024)S(1)}, f32[1536]{0:T(1024)}, u32[]{:S(2)}) copy-start(f32[1536]{0:T(1024)} %param.14) | copy-start | bytes 18436
